TPU v7x, 32 devices: a whole 2x2x4 slice. The times are simulated.
32 devices in a mesh: rows: 8 (over z, x), feat: 4 (over y, core).
Axes of the slice: x: 2, y: 2, z: 4, core: 2. Of those that a mesh axis runs over, the one named last changes fastest.
Arguments:
- tile_values: bfloat16 [2048, 256, 128], P('rows', 'feat'), may hold values from -6 to 6
- tile_blocks: int32 [2048, 256], P('rows', 'feat'), may hold values from 0 to 2047
- tile_counts: int32 [2048, 4], P('rows', 'feat'), may hold values from 1 to 64, as said below
- labels: int32 [2048], P('rows'), may hold values 0 or 1
- owner_rank: int32 [2048], P('rows'), may hold values from 0 to 7, as said below
- weights: float32 [8192, 128], P(('feat', 'rows')), may hold values from -0.09375 to 0.09375
Outputs:
- owned_margins: float32 [2048], P('rows')
- gradient: float32 [8192, 128], P(('feat', 'rows'))
- loss: float32 [], replicated
Inputs may be any that keep to these rules, and one draw needn't show every extreme that they name: `owner_rank`: within each aligned block of 256 examples, every owner is named by exactly 32 examples. `tile_counts`: in every aligned block of 256 examples, each shard's column holds at least one example with exactly 64 used slots.
All inputs are finite; a program needn't handle non-finite values. No bound on the sum of `labels` on one device may be relied on, other than what follows from the above.
Results may differ from a plain program's by a relative error of at most 0.003.
Values may be sent and summed in bfloat16 or wider, within the bound.
A program may use at most 64 MiB of HBM per device.

v0:
```python
import math
import jax
import jax.numpy as jnp
from jax import lax
from jax.sharding import PartitionSpec as P


def on_device(tile_values, tile_blocks, tile_counts, labels, owner_rank, weights):
    examples = tile_values.shape[0]
    slot_count = tile_values.shape[1]
    tile_width = tile_values.shape[2]
    peer_count = lax.axis_size("rows")
    per_owner = examples // peer_count
    w_half = weights.astype(jnp.bfloat16)
    weight_table = lax.all_gather(w_half, "rows", axis=0, tiled=True)
    owner_hits = (owner_rank[:, None] == jnp.arange(peer_count, dtype=jnp.int32)[None, :]).astype(
        jnp.int32
    )
    earlier = jnp.cumsum(owner_hits, axis=0) - owner_hits
    local_rank = jnp.sum(earlier * owner_hits, axis=1)
    position = owner_rank * per_owner + local_rank
    send_order = (
        jnp.zeros((examples,), jnp.int32).at[position].set(jnp.arange(examples, dtype=jnp.int32))
    )
    counts_here = tile_counts[:, 0]
    live_slot = jnp.arange(slot_count, dtype=jnp.int32)[None, :] < counts_here[:, None]
    picked = weight_table[tile_blocks]
    products = jnp.sum(tile_values.astype(jnp.float32) * picked.astype(jnp.float32), axis=2)
    partial_value = jnp.sum(jnp.where(live_slot, products, jnp.float32(0.0)), axis=1)
    margin = lax.psum(partial_value, "feat")
    label_float = labels.astype(jnp.float32)
    residual = jax.nn.sigmoid(margin) - label_float
    loss_terms = jnp.sum(jax.nn.softplus(margin) - label_float * margin)
    loss = lax.psum(loss_terms, "rows") / (examples * peer_count)
    resid_half = residual.astype(jnp.bfloat16)
    coefficient = jnp.where(live_slot, resid_half[:, None], jnp.zeros((), jnp.bfloat16))
    total_tiles = examples * slot_count
    block_rows = math.gcd(total_tiles, 1024)
    turn_count = total_tiles // block_rows
    flat_values = tile_values.reshape(turn_count, block_rows, tile_width)
    flat_blocks = tile_blocks.reshape(turn_count, block_rows)
    flat_coefficient = coefficient.reshape(turn_count, block_rows)
    row_count = weights.shape[0] * lax.axis_size("rows")
    candidates = jnp.arange(row_count, dtype=jnp.int32)

    def add_block(running, pieces):
        block_values, block_ids, block_coefficient = pieces
        matches = block_ids[:, None] == candidates[None, :]
        spread = jnp.where(matches, block_coefficient[:, None], jnp.zeros((), jnp.bfloat16))
        update = lax.dot_general(
            spread, block_values, (((0,), (0,)), ((), ())), preferred_element_type=jnp.float32
        )
        return (running + update, None)

    start_sum = jnp.zeros((row_count, tile_width), jnp.float32)
    summed, unused = lax.scan(add_block, start_sum, (flat_values, flat_blocks, flat_coefficient))
    gradient = lax.psum_scatter(summed, "rows", scatter_dimension=0, tiled=True)
    ordered = margin[send_order].reshape(peer_count, per_owner)
    owned_margins = lax.all_to_all(
        ordered, "rows", split_axis=0, concat_axis=0, tiled=True
    ).reshape(examples)
    return (owned_margins, gradient, loss)


def solution(mesh):
    in_specs = (
        P("rows", "feat", None),
        P("rows", "feat"),
        P("rows", "feat"),
        P("rows"),
        P("rows"),
        P(("feat", "rows"), None),
    )
    out_specs = (P("rows"), P(("feat", "rows"), None), P())
    return jax.shard_map(
        on_device, mesh=mesh, in_specs=in_specs, out_specs=out_specs, check_vma=False
    )
```

profile of v0, /device:TPU:0, one launch (start us, length us, event | category | flops | bytes accessed | tf_op | source)
XLA Modules:
  0.0 238.3 jit_solution(4810306240248693229)
XLA Ops:
  7.2 0.9 compare_select_fusion
  8.1 0.9 copy.16
  9.0 0.9 convert_element_type.23
  9.9 33.0 %all_gather.3 = bf16[2048,128]{1,0:T(8,128)(2,1)S(1)} all-gather(bf16[256,128]{1,0:T(8,128)(2,1)S(1)} %convert_element_type.23), channel_id=1, replica_groups=mesh['rows'=8,'feat'=4] {'rows'}, dimensions={0}, use_global_device_ids=true | all-gather | bytes 589824 | tf_op jit(solution)/shard_map/all_gather | solution.py:15
  43.0 0.1 copy.14
  43.2 57.4 %gather_fusion = bf16[16384,128]{1,0:T(8,128)(2,1)} fusion(bf16[2048,128]{1,0:T(8,128)(2,1)S(1)} %all_gather.3, s32[16384]{0:T(1024)S(1)} %broadcast_clamp_fusion), kind=kCustom, calls=%fused_computation | custom fusion | bytes 8454144 | tf_op jit(solution)/shard_map/gather | solution.py:27
  100.6 5.7 %fusion.15 = f32[256,64]{1,0:T(8,128)S(1)} fusion(bf16[256,64,128]{2,1,0:T(8,128)(2,1)} %bitcast.22, bf16[256,64,128]{2,1,0:T(8,128)(2,1)} %param.8), kind=kLoop, calls=%fused_computation.18 | loop fusion | flops 8372224 | bytes 8454144 | tf_op jit(solution)/shard_map/reduce_sum | solution.py:28
  106.3 0.2 select_reduce_fusion
  106.5 5.7 %psum.14 = f32[256]{0:T(256)S(1)} all-reduce(f32[256]{0:T(256)S(1)} %select_reduce_fusion), channel_id=1, replica_groups=mesh['rows'=8,'feat'=4] {'feat'}, use_global_device_ids=true, to_apply=%region_2.3 | all-reduce | flops 256 | bytes 2048 | tf_op jit(solution)/shard_map/psum | solution.py:30
  112.2 0.1 reshape.52
  112.3 0.6 fusion.20
  112.9 0.1 broadcast_in_dim.58
  113.0 0.1 broadcast_in_dim.59
  113.1 0.1 broadcast_in_dim.60
  113.2 0.5 broadcast.67
  113.7 0.7 reduce.11
  114.5 0.1 lt.57
  114.6 0.1 lt.58
  114.8 48.5 %while.11 = (s32[]{:T(128)}, f32[2048,128]{1,0:T(8,128)S(1)}, s32[16,1024]{1,0:T(8,128)S(1)}, bf16[16,1024]{1,0:T(8,128)(2,1)S(1)}, bf16[16,1024,128]{2,1,0:T(8,128)(2,1)}, /*index=5*/s32[]{:T(128)}, s32[]{:T(128)}) while((s32[]{:T(128)}, f32[2048,128]{1,0:T(8,128)S(1)}, s32[16,1024]{1,0:T(8,128)S(1)}, ...), condition=%wide.region_8.9_spmd.clone, body=%wide.region_7.8_spmd.clone.sunk | while | flops 541589504 | bytes 2377835 | solution.py:56
  114.9 3.0 %fusion.29 = f32[2048,128]{1,0:T(8,128)S(1)} fusion(s32[1024]{0:T(1024)S(1)} %bitcast.24, bf16[1024]{0:T(1024)(128)(2,1)S(1)} %dynamic-slice_reduce_fusion.2, f32[2048,128]{1,0:T(8,128)S(1)} %get-tuple-element.107, pred[]{:T(512)S(6)} %compare.3, bf16[16,1024,128]{2,1,0:T(8,128)(2,1)} %get-tuple-element.117, s32[]{:T(128)S(6)} %copy.20), kind=kOutput, calls=%fused_computation.8.clone.1 | convolution fusion | flops 541589504 | bytes 2365445 | tf_op jit(solution)/shard_map/while/body/eval_jaxpr/dot_general | solution.py:50
  117.9 3.0 %fusion.29 = f32[2048,128]{1,0:T(8,128)S(1)} fusion(s32[1024]{0:T(1024)S(1)} %bitcast.24, bf16[1024]{0:T(1024)(128)(2,1)S(1)} %dynamic-slice_reduce_fusion.2, f32[2048,128]{1,0:T(8,128)S(1)} %get-tuple-element.107, pred[]{:T(512)S(6)} %compare.3, bf16[16,1024,128]{2,1,0:T(8,128)(2,1)} %get-tuple-element.117, s32[]{:T(128)S(6)} %copy.20), kind=kOutput, calls=%fused_computation.8.clone.1 | convolution fusion | flops 541589504 | bytes 2365445 | tf_op jit(solution)/shard_map/while/body/eval_jaxpr/dot_general | solution.py:50
  120.9 3.0 %fusion.29 = f32[2048,128]{1,0:T(8,128)S(1)} fusion(s32[1024]{0:T(1024)S(1)} %bitcast.24, bf16[1024]{0:T(1024)(128)(2,1)S(1)} %dynamic-slice_reduce_fusion.2, f32[2048,128]{1,0:T(8,128)S(1)} %get-tuple-element.107, pred[]{:T(512)S(6)} %compare.3, bf16[16,1024,128]{2,1,0:T(8,128)(2,1)} %get-tuple-element.117, s32[]{:T(128)S(6)} %copy.20), kind=kOutput, calls=%fused_computation.8.clone.1 | convolution fusion | flops 541589504 | bytes 2365445 | tf_op jit(solution)/shard_map/while/body/eval_jaxpr/dot_general | solution.py:50
  123.9 3.0 %fusion.29 = f32[2048,128]{1,0:T(8,128)S(1)} fusion(s32[1024]{0:T(1024)S(1)} %bitcast.24, bf16[1024]{0:T(1024)(128)(2,1)S(1)} %dynamic-slice_reduce_fusion.2, f32[2048,128]{1,0:T(8,128)S(1)} %get-tuple-element.107, pred[]{:T(512)S(6)} %compare.3, bf16[16,1024,128]{2,1,0:T(8,128)(2,1)} %get-tuple-element.117, s32[]{:T(128)S(6)} %copy.20), kind=kOutput, calls=%fused_computation.8.clone.1 | convolution fusion | flops 541589504 | bytes 2365445 | tf_op jit(solution)/shard_map/while/body/eval_jaxpr/dot_general | solution.py:50
  127.0 3.0 %fusion.29 = f32[2048,128]{1,0:T(8,128)S(1)} fusion(s32[1024]{0:T(1024)S(1)} %bitcast.24, bf16[1024]{0:T(1024)(128)(2,1)S(1)} %dynamic-slice_reduce_fusion.2, f32[2048,128]{1,0:T(8,128)S(1)} %get-tuple-element.107, pred[]{:T(512)S(6)} %compare.3, bf16[16,1024,128]{2,1,0:T(8,128)(2,1)} %get-tuple-element.117, s32[]{:T(128)S(6)} %copy.20), kind=kOutput, calls=%fused_computation.8.clone.1 | convolution fusion | flops 541589504 | bytes 2365445 | tf_op jit(solution)/shard_map/while/body/eval_jaxpr/dot_general | solution.py:50
  130.0 3.0 %fusion.29 = f32[2048,128]{1,0:T(8,128)S(1)} fusion(s32[1024]{0:T(1024)S(1)} %bitcast.24, bf16[1024]{0:T(1024)(128)(2,1)S(1)} %dynamic-slice_reduce_fusion.2, f32[2048,128]{1,0:T(8,128)S(1)} %get-tuple-element.107, pred[]{:T(512)S(6)} %compare.3, bf16[16,1024,128]{2,1,0:T(8,128)(2,1)} %get-tuple-element.117, s32[]{:T(128)S(6)} %copy.20), kind=kOutput, calls=%fused_computation.8.clone.1 | convolution fusion | flops 541589504 | bytes 2365445 | tf_op jit(solution)/shard_map/while/body/eval_jaxpr/dot_general | solution.py:50
  133.0 3.0 %fusion.29 = f32[2048,128]{1,0:T(8,128)S(1)} fusion(s32[1024]{0:T(1024)S(1)} %bitcast.24, bf16[1024]{0:T(1024)(128)(2,1)S(1)} %dynamic-slice_reduce_fusion.2, f32[2048,128]{1,0:T(8,128)S(1)} %get-tuple-element.107, pred[]{:T(512)S(6)} %compare.3, bf16[16,1024,128]{2,1,0:T(8,128)(2,1)} %get-tuple-element.117, s32[]{:T(128)S(6)} %copy.20), kind=kOutput, calls=%fused_computation.8.clone.1 | convolution fusion | flops 541589504 | bytes 2365445 | tf_op jit(solution)/shard_map/while/body/eval_jaxpr/dot_general | solution.py:50
  136.1 3.0 %fusion.29 = f32[2048,128]{1,0:T(8,128)S(1)} fusion(s32[1024]{0:T(1024)S(1)} %bitcast.24, bf16[1024]{0:T(1024)(128)(2,1)S(1)} %dynamic-slice_reduce_fusion.2, f32[2048,128]{1,0:T(8,128)S(1)} %get-tuple-element.107, pred[]{:T(512)S(6)} %compare.3, bf16[16,1024,128]{2,1,0:T(8,128)(2,1)} %get-tuple-element.117, s32[]{:T(128)S(6)} %copy.20), kind=kOutput, calls=%fused_computation.8.clone.1 | convolution fusion | flops 541589504 | bytes 2365445 | tf_op jit(solution)/shard_map/while/body/eval_jaxpr/dot_general | solution.py:50
  139.1 3.0 %fusion.29 = f32[2048,128]{1,0:T(8,128)S(1)} fusion(s32[1024]{0:T(1024)S(1)} %bitcast.24, bf16[1024]{0:T(1024)(128)(2,1)S(1)} %dynamic-slice_reduce_fusion.2, f32[2048,128]{1,0:T(8,128)S(1)} %get-tuple-element.107, pred[]{:T(512)S(6)} %compare.3, bf16[16,1024,128]{2,1,0:T(8,128)(2,1)} %get-tuple-element.117, s32[]{:T(128)S(6)} %copy.20), kind=kOutput, calls=%fused_computation.8.clone.1 | convolution fusion | flops 541589504 | bytes 2365445 | tf_op jit(solution)/shard_map/while/body/eval_jaxpr/dot_general | solution.py:50
  142.1 3.0 %fusion.29 = f32[2048,128]{1,0:T(8,128)S(1)} fusion(s32[1024]{0:T(1024)S(1)} %bitcast.24, bf16[1024]{0:T(1024)(128)(2,1)S(1)} %dynamic-slice_reduce_fusion.2, f32[2048,128]{1,0:T(8,128)S(1)} %get-tuple-element.107, pred[]{:T(512)S(6)} %compare.3, bf16[16,1024,128]{2,1,0:T(8,128)(2,1)} %get-tuple-element.117, s32[]{:T(128)S(6)} %copy.20), kind=kOutput, calls=%fused_computation.8.clone.1 | convolution fusion | flops 541589504 | bytes 2365445 | tf_op jit(solution)/shard_map/while/body/eval_jaxpr/dot_general | solution.py:50
  145.2 3.0 %fusion.29 = f32[2048,128]{1,0:T(8,128)S(1)} fusion(s32[1024]{0:T(1024)S(1)} %bitcast.24, bf16[1024]{0:T(1024)(128)(2,1)S(1)} %dynamic-slice_reduce_fusion.2, f32[2048,128]{1,0:T(8,128)S(1)} %get-tuple-element.107, pred[]{:T(512)S(6)} %compare.3, bf16[16,1024,128]{2,1,0:T(8,128)(2,1)} %get-tuple-element.117, s32[]{:T(128)S(6)} %copy.20), kind=kOutput, calls=%fused_computation.8.clone.1 | convolution fusion | flops 541589504 | bytes 2365445 | tf_op jit(solution)/shard_map/while/body/eval_jaxpr/dot_general | solution.py:50
  148.2 3.0 %fusion.29 = f32[2048,128]{1,0:T(8,128)S(1)} fusion(s32[1024]{0:T(1024)S(1)} %bitcast.24, bf16[1024]{0:T(1024)(128)(2,1)S(1)} %dynamic-slice_reduce_fusion.2, f32[2048,128]{1,0:T(8,128)S(1)} %get-tuple-element.107, pred[]{:T(512)S(6)} %compare.3, bf16[16,1024,128]{2,1,0:T(8,128)(2,1)} %get-tuple-element.117, s32[]{:T(128)S(6)} %copy.20), kind=kOutput, calls=%fused_computation.8.clone.1 | convolution fusion | flops 541589504 | bytes 2365445 | tf_op jit(solution)/shard_map/while/body/eval_jaxpr/dot_general | solution.py:50
  151.2 3.0 %fusion.29 = f32[2048,128]{1,0:T(8,128)S(1)} fusion(s32[1024]{0:T(1024)S(1)} %bitcast.24, bf16[1024]{0:T(1024)(128)(2,1)S(1)} %dynamic-slice_reduce_fusion.2, f32[2048,128]{1,0:T(8,128)S(1)} %get-tuple-element.107, pred[]{:T(512)S(6)} %compare.3, bf16[16,1024,128]{2,1,0:T(8,128)(2,1)} %get-tuple-element.117, s32[]{:T(128)S(6)} %copy.20), kind=kOutput, calls=%fused_computation.8.clone.1 | convolution fusion | flops 541589504 | bytes 2365445 | tf_op jit(solution)/shard_map/while/body/eval_jaxpr/dot_general | solution.py:50
  154.3 3.0 %fusion.29 = f32[2048,128]{1,0:T(8,128)S(1)} fusion(s32[1024]{0:T(1024)S(1)} %bitcast.24, bf16[1024]{0:T(1024)(128)(2,1)S(1)} %dynamic-slice_reduce_fusion.2, f32[2048,128]{1,0:T(8,128)S(1)} %get-tuple-element.107, pred[]{:T(512)S(6)} %compare.3, bf16[16,1024,128]{2,1,0:T(8,128)(2,1)} %get-tuple-element.117, s32[]{:T(128)S(6)} %copy.20), kind=kOutput, calls=%fused_computation.8.clone.1 | convolution fusion | flops 541589504 | bytes 2365445 | tf_op jit(solution)/shard_map/while/body/eval_jaxpr/dot_general | solution.py:50
  157.3 3.0 %fusion.29 = f32[2048,128]{1,0:T(8,128)S(1)} fusion(s32[1024]{0:T(1024)S(1)} %bitcast.24, bf16[1024]{0:T(1024)(128)(2,1)S(1)} %dynamic-slice_reduce_fusion.2, f32[2048,128]{1,0:T(8,128)S(1)} %get-tuple-element.107, pred[]{:T(512)S(6)} %compare.3, bf16[16,1024,128]{2,1,0:T(8,128)(2,1)} %get-tuple-element.117, s32[]{:T(128)S(6)} %copy.20), kind=kOutput, calls=%fused_computation.8.clone.1 | convolution fusion | flops 541589504 | bytes 2365445 | tf_op jit(solution)/shard_map/while/body/eval_jaxpr/dot_general | solution.py:50
  160.3 3.0 %fusion.29 = f32[2048,128]{1,0:T(8,128)S(1)} fusion(s32[1024]{0:T(1024)S(1)} %bitcast.24, bf16[1024]{0:T(1024)(128)(2,1)S(1)} %dynamic-slice_reduce_fusion.2, f32[2048,128]{1,0:T(8,128)S(1)} %get-tuple-element.107, pred[]{:T(512)S(6)} %compare.3, bf16[16,1024,128]{2,1,0:T(8,128)(2,1)} %get-tuple-element.117, s32[]{:T(128)S(6)} %copy.20), kind=kOutput, calls=%fused_computation.8.clone.1 | convolution fusion | flops 541589504 | bytes 2365445 | tf_op jit(solution)/shard_map/while/body/eval_jaxpr/dot_general | solution.py:50
  163.3 1.0 copy-done
  164.3 0.6 reduce-window.6
  164.9 0.2 slice_reduce_fusion
  165.2 0.1 fusion.17
  165.3 1.4 scatter_custom_fusion
  166.7 1.9 gather_fusion.1
  168.7 0.7 all_to_all.6
  169.4 5.6 %all-to-all-start = ((f32[8,1,32]{2,1,0:T(1,128)}), f32[8,1,32]{2,1,0:T(1,128)S(1)}, u32[]{:S(2)}, u32[]{:S(2)}) async-start(f32[8,1,32]{2,1,0:T(1,128)} %all_to_all.6), calls=%async_computation | async-start | bytes 8192 | tf_op jit(solution)/shard_map/all_to_all | solution.py:59
  175.0 22.5 %psum.15 = f32[]{:T(128)} all-reduce(f32[]{:T(128)} %get-tuple-element.66), channel_id=1, replica_groups=mesh['rows'=8,'feat'=4] {'rows'}, use_global_device_ids=true, to_apply=%region_11.12 | all-reduce | flops 1 | bytes 8 | tf_op jit(solution)/shard_map/psum | solution.py:34
  198.1 0.5 broadcast.66
  198.6 0.7 reduce.10
  199.3 0.6 reshape.51
  199.9 30.4 %reduce-scatter.2.cloned.1.call-done = f32[256,128]{1,0:T(8,128)} async-done(((f32[2048,128]{1,0:T(8,128)}), f32[256,128]{1,0:T(8,128)}) %reduce-scatter.2.cloned.1.call-update) | async-done | bytes 131088 | tf_op jit(solution)/shard_map/reduce_scatter | solution.py:57
  (56 shorter events, 1.1 us)
Async XLA Ops:
  7.2 223.2 %reduce-scatter.2.cloned.1.call-start = ((), (), s32[]{:S(2)}) async-start(), calls=%async_computation.2 | async-start | bytes 1179648 | tf_op jit(solution)/shard_map/reduce_scatter | solution.py:57
  100.6 5.7 %copy-start.2 = (s32[256,1]{0,1:T(1,128)S(1)}, s32[256,1]{0,1:T(1,128)}, u32[]{:S(2)}) copy-start(s32[256,1]{0,1:T(1,128)} %param.10) | copy-start | bytes 3076
  100.6 11.7 %copy-start.3 = (s32[256]{0:T(256)S(1)}, s32[256]{0:T(256)}, u32[]{:S(2)}) copy-start(s32[256]{0:T(256)} %param.11) | copy-start | bytes 3076
  114.8 49.5 %copy-start.1 = (s32[256]{0:T(256)S(1)}, s32[256]{0:T(256)}, u32[]{:S(2)}) copy-start(s32[256]{0:T(256)} %param.12) | copy-start | bytes 3076
  163.3 1.0 copy-start
  169.4 28.7 %all-to-all-start = ((f32[8,1,32]{2,1,0:T(1,128)}), f32[8,1,32]{2,1,0:T(1,128)S(1)}, u32[]{:S(2)}, u32[]{:S(2)}) async-start(f32[8,1,32]{2,1,0:T(1,128)} %all_to_all.6), calls=%async_computation | async-start | bytes 8192 | tf_op jit(solution)/shard_map/all_to_all | solution.py:59
Sparse Core Ops, SparseCore 0:
  164.4 65.8 reduce-scatter.1
where the time goes:
time: 239 us; the launch traced here: 238 us
  local copies, waits for them, and re-layouts  66.9 us (28%)
  blocking collectives  61.2 us (26%)
  matrix products  47.2 us (20%)
  waiting for transfers between devices  30.4 us (13%)
  between operations  16 us (7%)
  other arithmetic  10.4 us (4%)
  starting transfers between devices  5.66 us (2%)
    gather x1, local copies, waits for them, and re-layouts, on_device(): picked = weight_table[tile_blocks]  57.4 us
    dot_general x16, matrix products, add_block(): lax.dot_general(spread, block_values, (((0,), (0,)), ((), ())), preferred...  47.2 us
    all_gather x1, blocking collectives, on_device(): weight_table = lax.all_gather(w_half, 'rows', axis=0, tiled=True)  33 us
    reduce_scatter x1, waiting for transfers between devices, on_device(): gradient = lax.psum_scatter(summed, 'rows', scatter_dimension=0, tiled=True)  30.4 us
    psum x1, blocking collectives, on_device(): loss = lax.psum(loss_terms, 'rows') / (examples * peer_count)  22.5 us
    reduce_sum x1, other arithmetic, on_device(): jnp.sum(tile_values.astype(jnp.float32) * picked.astype(jnp.float32), axi...  5.72 us
    psum x1, blocking collectives, on_device(): margin = lax.psum(partial_value, 'feat')  5.66 us
    all_to_all x1, starting transfers between devices, on_device(): lax.all_to_all(ordered, 'rows', split_axis=0, concat_axis=0, tiled=True)  5.62 us
  transfers between devices with their start and end apart: 2, of which 1 were waited for; matrix products, arithmetic and copies ran while one was open for 3% of the time, Pallas kernels for 0%

commit v1 on v0

--- a/solution.py
+++ b/solution.py
@@ -12,7 +12,12 @@
     peer_count = lax.axis_size("rows")
     per_owner = examples // peer_count
     w_half = weights.astype(jnp.bfloat16)
-    weight_table = lax.all_gather(w_half, "rows", axis=0, tiled=True)
+    ring = [w_half]
+    for hop in range(7):
+        ring.append(lax.ppermute(ring[-1], "rows", [(dev, (dev + 1) % 8) for dev in range(8)]))
+    weight_table = jnp.roll(
+        jnp.concatenate(ring[::-1], axis=0), (lax.axis_index("rows") + 1) * ring[0].shape[0], axis=0
+    )
     owner_hits = (owner_rank[:, None] == jnp.arange(peer_count, dtype=jnp.int32)[None, :]).astype(
         jnp.int32
     )

time: 239 us -> 252 us (1.054)
  waiting for transfers between devices: 30.4 us -> 72.8 us
  blocking collectives: 61.2 us -> 28.1 us
    ppermute x0 -> x7, waiting for transfers between devices: none -> 43 us  [on_device(): lax.ppermute(ring[-1], 'rows', [(dev, (dev + 1) % 8) for dev in range(8)])]
    all_gather x1 -> x0, blocking collectives: 33 us -> none  [on_device(): weight_table = lax.all_gather(w_half, 'rows', axis=0, tiled=True)]
    ppermute x0 -> x7, starting transfers between devices: none -> 2.98 us  [on_device(): lax.ppermute(ring[-1], 'rows', [(dev, (dev + 1) % 8) for dev in range(8)])]
  transfers between devices with their start and end apart: 2 -> 9, of which waited for: 1 -> 8; matrix products, arithmetic and copies ran while one was open for 3% -> 4% of each run, Pallas kernels for 0% -> 0%
where the time goes in v1:
time: 252 us; the launch traced here: 251 us
  waiting for transfers between devices  72.8 us (29%)
  local copies, waits for them, and re-layouts  67 us (27%)
  matrix products  47 us (19%)
  blocking collectives  28.1 us (11%)
  between operations  16.1 us (6%)
  other arithmetic  12.9 us (5%)
  starting transfers between devices  6.35 us (3%)
    gather x1, local copies, waits for them, and re-layouts, on_device(): picked = weight_table[tile_blocks]  57.4 us
    dot_general x16, matrix products, add_block(): lax.dot_general(spread, block_values, (((0,), (0,)), ((), ())), preferred...  47 us
    ppermute x7, waiting for transfers between devices, on_device(): lax.ppermute(ring[-1], 'rows', [(dev, (dev + 1) % 8) for dev in range(8)])  43 us
    reduce_scatter x1, waiting for transfers between devices, on_device(): gradient = lax.psum_scatter(summed, 'rows', scatter_dimension=0, tiled=True)  29.8 us
    psum x1, blocking collectives, on_device(): loss = lax.psum(loss_terms, 'rows') / (examples * peer_count)  22.4 us
    reduce_sum x1, other arithmetic, on_device(): jnp.sum(tile_values.astype(jnp.float32) * picked.astype(jnp.float32), axi...  5.72 us
    psum x1, blocking collectives, on_device(): margin = lax.psum(partial_value, 'feat')  5.66 us
  transfers between devices with their start and end apart: 9, of which 8 were waited for; matrix products, arithmetic and copies ran while one was open for 4% of the time, Pallas kernels for 0%

profile of v1, /device:TPU:0, one launch (start us, length us, event | category | flops | bytes accessed | tf_op | source)
XLA Modules:
  0.0 250.9 jit_solution(12156957905700008809)
XLA Ops:
  7.2 0.9 convert_element_type.23
  8.1 3.0 %collective-permute-start = (bf16[256,128]{1,0:T(8,128)(2,1)S(1)}, bf16[256,128]{1,0:T(8,128)(2,1)S(1)}, u32[]{:S(2)}, u32[]{:S(2)}) collective-permute-start(bf16[256,128]{1,0:T(8,128)(2,1)S(1)} %convert_element_type.23), channel_id=1, source_target_pairs={{0,4},{4,8},{8,12},{12,16},{16,20},{20,24},{24,28},{28,0},{1,5},{5... | collective-permute-start | bytes 196616 | tf_op jit(solution)/shard_map/ppermute | solution.py:17
  11.1 5.3 %collective-permute-done = bf16[256,128]{1,0:T(8,128)(2,1)S(1)} collective-permute-done((bf16[256,128]{1,0:T(8,128)(2,1)S(1)}, bf16[256,128]{1,0:T(8,128)(2,1)S(1)}, u32[]{:S(2)}, u32[]{:S(2)}) %collective-permute-start) | collective-permute-done | bytes 65568 | tf_op jit(solution)/shard_map/ppermute | solution.py:17
  16.4 7.0 %collective-permute-done.1 = bf16[256,128]{1,0:T(8,128)(2,1)S(1)} collective-permute-done((bf16[256,128]{1,0:T(8,128)(2,1)S(1)}, bf16[256,128]{1,0:T(8,128)(2,1)S(1)}, u32[]{:S(2)}, u32[]{:S(2)}) %collective-permute-start.1) | collective-permute-done | bytes 65568 | tf_op jit(solution)/shard_map/ppermute | solution.py:17
  23.3 7.0 %collective-permute-done.2 = bf16[256,128]{1,0:T(8,128)(2,1)S(1)} collective-permute-done((bf16[256,128]{1,0:T(8,128)(2,1)S(1)}, bf16[256,128]{1,0:T(8,128)(2,1)S(1)}, u32[]{:S(2)}, u32[]{:S(2)}) %collective-permute-start.2) | collective-permute-done | bytes 65568 | tf_op jit(solution)/shard_map/ppermute | solution.py:17
  30.3 7.0 %collective-permute-done.3 = bf16[256,128]{1,0:T(8,128)(2,1)S(1)} collective-permute-done((bf16[256,128]{1,0:T(8,128)(2,1)S(1)}, bf16[256,128]{1,0:T(8,128)(2,1)S(1)}, u32[]{:S(2)}, u32[]{:S(2)}) %collective-permute-start.3) | collective-permute-done | bytes 65568 | tf_op jit(solution)/shard_map/ppermute | solution.py:17
  37.3 7.3 %collective-permute-done.4 = bf16[256,128]{1,0:T(8,128)(2,1)S(1)} collective-permute-done((bf16[256,128]{1,0:T(8,128)(2,1)S(1)}, bf16[256,128]{1,0:T(8,128)(2,1)S(1)}, u32[]{:S(2)}, u32[]{:S(2)}) %collective-permute-start.4) | collective-permute-done | bytes 65568 | tf_op jit(solution)/shard_map/ppermute | solution.py:17
  44.6 0.8 compare_select_fusion
  45.6 5.9 %collective-permute-done.5 = bf16[256,128]{1,0:T(8,128)(2,1)S(1)} collective-permute-done((bf16[256,128]{1,0:T(8,128)(2,1)S(1)}, bf16[256,128]{1,0:T(8,128)(2,1)S(1)}, u32[]{:S(2)}, u32[]{:S(2)}) %collective-permute-start.5) | collective-permute-done | bytes 65568 | tf_op jit(solution)/shard_map/ppermute | solution.py:17
  51.6 0.9 copy.16
  52.5 0.5 broadcast.68
  53.0 1.3 reduce.11
  54.8 3.7 %collective-permute-done.6 = bf16[256,128]{1,0:T(8,128)(2,1)S(1)} collective-permute-done((bf16[256,128]{1,0:T(8,128)(2,1)S(1)}, bf16[256,128]{1,0:T(8,128)(2,1)S(1)}, u32[]{:S(2)}, u32[]{:S(2)}) %collective-permute-start.6) | collective-permute-done | bytes 65568 | tf_op jit(solution)/shard_map/ppermute | solution.py:17
  58.6 0.9 constant_dynamic-update-slice_fusion.8
  59.7 0.9 constant_dynamic-update-slice_fusion
  60.6 57.4 %gather_fusion = bf16[16384,128]{1,0:T(8,128)(2,1)} fusion(bf16[2048,128]{1,0:T(8,128)(2,1)S(1)} %constant_dynamic-slice_fusion.1, s32[16384]{0:T(1024)S(1)} %broadcast_clamp_fusion), kind=kCustom, calls=%fused_computation | custom fusion | bytes 8454144 | tf_op jit(solution)/shard_map/gather | solution.py:32
  118.0 5.7 %fusion.15 = f32[256,64]{1,0:T(8,128)S(1)} fusion(bf16[256,64,128]{2,1,0:T(8,128)(2,1)} %bitcast.22, bf16[256,64,128]{2,1,0:T(8,128)(2,1)} %param.8), kind=kLoop, calls=%fused_computation.18 | loop fusion | flops 8372224 | bytes 8454144 | tf_op jit(solution)/shard_map/reduce_sum | solution.py:33
  123.9 5.7 %psum.14 = f32[256]{0:T(256)S(1)} all-reduce(f32[256]{0:T(256)S(1)} %select_reduce_fusion), channel_id=1, replica_groups=mesh['rows'=8,'feat'=4] {'feat'}, use_global_device_ids=true, to_apply=%region_2.3 | all-reduce | flops 256 | bytes 2048 | tf_op jit(solution)/shard_map/psum | solution.py:35
  129.6 0.6 fusion.20
  130.6 48.3 %while.11 = (s32[]{:T(128)}, f32[2048,128]{1,0:T(8,128)S(1)}, s32[16,1024]{1,0:T(8,128)S(1)}, bf16[16,1024]{1,0:T(8,128)(2,1)S(1)}, bf16[16,1024,128]{2,1,0:T(8,128)(2,1)}, /*index=5*/s32[]{:T(128)}, s32[]{:T(128)}) while((s32[]{:T(128)}, f32[2048,128]{1,0:T(8,128)S(1)}, s32[16,1024]{1,0:T(8,128)S(1)}, ...), condition=%wide.region_8.9_spmd.clone, body=%wide.region_7.8_spmd.clone.sunk | while | flops 541589504 | bytes 2378335 | solution.py:61
  130.6 2.9 %fusion.29 = f32[2048,128]{1,0:T(8,128)S(1)} fusion(s32[1024]{0:T(1024)S(1)} %bitcast.24, bf16[1024]{0:T(1024)(128)(2,1)S(1)} %dynamic-slice_reduce_fusion.2, f32[2048,128]{1,0:T(8,128)S(1)} %get-tuple-element.107, pred[]{:T(512)S(6)} %compare.4, bf16[16,1024,128]{2,1,0:T(8,128)(2,1)} %get-tuple-element.117, s32[]{:T(128)} %get-tuple-element.106), kind=kOutput, calls=%fused_computation.8.clone.1 | convolution fusion | flops 541589504 | bytes 2365953 | tf_op jit(solution)/shard_map/while/body/eval_jaxpr/dot_general | solution.py:55
  133.7 2.9 %fusion.29 = f32[2048,128]{1,0:T(8,128)S(1)} fusion(s32[1024]{0:T(1024)S(1)} %bitcast.24, bf16[1024]{0:T(1024)(128)(2,1)S(1)} %dynamic-slice_reduce_fusion.2, f32[2048,128]{1,0:T(8,128)S(1)} %get-tuple-element.107, pred[]{:T(512)S(6)} %compare.4, bf16[16,1024,128]{2,1,0:T(8,128)(2,1)} %get-tuple-element.117, s32[]{:T(128)} %get-tuple-element.106), kind=kOutput, calls=%fused_computation.8.clone.1 | convolution fusion | flops 541589504 | bytes 2365953 | tf_op jit(solution)/shard_map/while/body/eval_jaxpr/dot_general | solution.py:55
  136.7 2.9 %fusion.29 = f32[2048,128]{1,0:T(8,128)S(1)} fusion(s32[1024]{0:T(1024)S(1)} %bitcast.24, bf16[1024]{0:T(1024)(128)(2,1)S(1)} %dynamic-slice_reduce_fusion.2, f32[2048,128]{1,0:T(8,128)S(1)} %get-tuple-element.107, pred[]{:T(512)S(6)} %compare.4, bf16[16,1024,128]{2,1,0:T(8,128)(2,1)} %get-tuple-element.117, s32[]{:T(128)} %get-tuple-element.106), kind=kOutput, calls=%fused_computation.8.clone.1 | convolution fusion | flops 541589504 | bytes 2365953 | tf_op jit(solution)/shard_map/while/body/eval_jaxpr/dot_general | solution.py:55
  139.7 2.9 %fusion.29 = f32[2048,128]{1,0:T(8,128)S(1)} fusion(s32[1024]{0:T(1024)S(1)} %bitcast.24, bf16[1024]{0:T(1024)(128)(2,1)S(1)} %dynamic-slice_reduce_fusion.2, f32[2048,128]{1,0:T(8,128)S(1)} %get-tuple-element.107, pred[]{:T(512)S(6)} %compare.4, bf16[16,1024,128]{2,1,0:T(8,128)(2,1)} %get-tuple-element.117, s32[]{:T(128)} %get-tuple-element.106), kind=kOutput, calls=%fused_computation.8.clone.1 | convolution fusion | flops 541589504 | bytes 2365953 | tf_op jit(solution)/shard_map/while/body/eval_jaxpr/dot_general | solution.py:55
  142.7 2.9 %fusion.29 = f32[2048,128]{1,0:T(8,128)S(1)} fusion(s32[1024]{0:T(1024)S(1)} %bitcast.24, bf16[1024]{0:T(1024)(128)(2,1)S(1)} %dynamic-slice_reduce_fusion.2, f32[2048,128]{1,0:T(8,128)S(1)} %get-tuple-element.107, pred[]{:T(512)S(6)} %compare.4, bf16[16,1024,128]{2,1,0:T(8,128)(2,1)} %get-tuple-element.117, s32[]{:T(128)} %get-tuple-element.106), kind=kOutput, calls=%fused_computation.8.clone.1 | convolution fusion | flops 541589504 | bytes 2365953 | tf_op jit(solution)/shard_map/while/body/eval_jaxpr/dot_general | solution.py:55
  145.7 2.9 %fusion.29 = f32[2048,128]{1,0:T(8,128)S(1)} fusion(s32[1024]{0:T(1024)S(1)} %bitcast.24, bf16[1024]{0:T(1024)(128)(2,1)S(1)} %dynamic-slice_reduce_fusion.2, f32[2048,128]{1,0:T(8,128)S(1)} %get-tuple-element.107, pred[]{:T(512)S(6)} %compare.4, bf16[16,1024,128]{2,1,0:T(8,128)(2,1)} %get-tuple-element.117, s32[]{:T(128)} %get-tuple-element.106), kind=kOutput, calls=%fused_computation.8.clone.1 | convolution fusion | flops 541589504 | bytes 2365953 | tf_op jit(solution)/shard_map/while/body/eval_jaxpr/dot_general | solution.py:55
  148.7 2.9 %fusion.29 = f32[2048,128]{1,0:T(8,128)S(1)} fusion(s32[1024]{0:T(1024)S(1)} %bitcast.24, bf16[1024]{0:T(1024)(128)(2,1)S(1)} %dynamic-slice_reduce_fusion.2, f32[2048,128]{1,0:T(8,128)S(1)} %get-tuple-element.107, pred[]{:T(512)S(6)} %compare.4, bf16[16,1024,128]{2,1,0:T(8,128)(2,1)} %get-tuple-element.117, s32[]{:T(128)} %get-tuple-element.106), kind=kOutput, calls=%fused_computation.8.clone.1 | convolution fusion | flops 541589504 | bytes 2365953 | tf_op jit(solution)/shard_map/while/body/eval_jaxpr/dot_general | solution.py:55
  151.8 2.9 %fusion.29 = f32[2048,128]{1,0:T(8,128)S(1)} fusion(s32[1024]{0:T(1024)S(1)} %bitcast.24, bf16[1024]{0:T(1024)(128)(2,1)S(1)} %dynamic-slice_reduce_fusion.2, f32[2048,128]{1,0:T(8,128)S(1)} %get-tuple-element.107, pred[]{:T(512)S(6)} %compare.4, bf16[16,1024,128]{2,1,0:T(8,128)(2,1)} %get-tuple-element.117, s32[]{:T(128)} %get-tuple-element.106), kind=kOutput, calls=%fused_computation.8.clone.1 | convolution fusion | flops 541589504 | bytes 2365953 | tf_op jit(solution)/shard_map/while/body/eval_jaxpr/dot_general | solution.py:55
  154.8 2.9 %fusion.29 = f32[2048,128]{1,0:T(8,128)S(1)} fusion(s32[1024]{0:T(1024)S(1)} %bitcast.24, bf16[1024]{0:T(1024)(128)(2,1)S(1)} %dynamic-slice_reduce_fusion.2, f32[2048,128]{1,0:T(8,128)S(1)} %get-tuple-element.107, pred[]{:T(512)S(6)} %compare.4, bf16[16,1024,128]{2,1,0:T(8,128)(2,1)} %get-tuple-element.117, s32[]{:T(128)} %get-tuple-element.106), kind=kOutput, calls=%fused_computation.8.clone.1 | convolution fusion | flops 541589504 | bytes 2365953 | tf_op jit(solution)/shard_map/while/body/eval_jaxpr/dot_general | solution.py:55
  157.8 2.9 %fusion.29 = f32[2048,128]{1,0:T(8,128)S(1)} fusion(s32[1024]{0:T(1024)S(1)} %bitcast.24, bf16[1024]{0:T(1024)(128)(2,1)S(1)} %dynamic-slice_reduce_fusion.2, f32[2048,128]{1,0:T(8,128)S(1)} %get-tuple-element.107, pred[]{:T(512)S(6)} %compare.4, bf16[16,1024,128]{2,1,0:T(8,128)(2,1)} %get-tuple-element.117, s32[]{:T(128)} %get-tuple-element.106), kind=kOutput, calls=%fused_computation.8.clone.1 | convolution fusion | flops 541589504 | bytes 2365953 | tf_op jit(solution)/shard_map/while/body/eval_jaxpr/dot_general | solution.py:55
  160.8 2.9 %fusion.29 = f32[2048,128]{1,0:T(8,128)S(1)} fusion(s32[1024]{0:T(1024)S(1)} %bitcast.24, bf16[1024]{0:T(1024)(128)(2,1)S(1)} %dynamic-slice_reduce_fusion.2, f32[2048,128]{1,0:T(8,128)S(1)} %get-tuple-element.107, pred[]{:T(512)S(6)} %compare.4, bf16[16,1024,128]{2,1,0:T(8,128)(2,1)} %get-tuple-element.117, s32[]{:T(128)} %get-tuple-element.106), kind=kOutput, calls=%fused_computation.8.clone.1 | convolution fusion | flops 541589504 | bytes 2365953 | tf_op jit(solution)/shard_map/while/body/eval_jaxpr/dot_general | solution.py:55
  163.8 2.9 %fusion.29 = f32[2048,128]{1,0:T(8,128)S(1)} fusion(s32[1024]{0:T(1024)S(1)} %bitcast.24, bf16[1024]{0:T(1024)(128)(2,1)S(1)} %dynamic-slice_reduce_fusion.2, f32[2048,128]{1,0:T(8,128)S(1)} %get-tuple-element.107, pred[]{:T(512)S(6)} %compare.4, bf16[16,1024,128]{2,1,0:T(8,128)(2,1)} %get-tuple-element.117, s32[]{:T(128)} %get-tuple-element.106), kind=kOutput, calls=%fused_computation.8.clone.1 | convolution fusion | flops 541589504 | bytes 2365953 | tf_op jit(solution)/shard_map/while/body/eval_jaxpr/dot_general | solution.py:55
  166.8 2.9 %fusion.29 = f32[2048,128]{1,0:T(8,128)S(1)} fusion(s32[1024]{0:T(1024)S(1)} %bitcast.24, bf16[1024]{0:T(1024)(128)(2,1)S(1)} %dynamic-slice_reduce_fusion.2, f32[2048,128]{1,0:T(8,128)S(1)} %get-tuple-element.107, pred[]{:T(512)S(6)} %compare.4, bf16[16,1024,128]{2,1,0:T(8,128)(2,1)} %get-tuple-element.117, s32[]{:T(128)} %get-tuple-element.106), kind=kOutput, calls=%fused_computation.8.clone.1 | convolution fusion | flops 541589504 | bytes 2365953 | tf_op jit(solution)/shard_map/while/body/eval_jaxpr/dot_general | solution.py:55
  169.9 2.9 %fusion.29 = f32[2048,128]{1,0:T(8,128)S(1)} fusion(s32[1024]{0:T(1024)S(1)} %bitcast.24, bf16[1024]{0:T(1024)(128)(2,1)S(1)} %dynamic-slice_reduce_fusion.2, f32[2048,128]{1,0:T(8,128)S(1)} %get-tuple-element.107, pred[]{:T(512)S(6)} %compare.4, bf16[16,1024,128]{2,1,0:T(8,128)(2,1)} %get-tuple-element.117, s32[]{:T(128)} %get-tuple-element.106), kind=kOutput, calls=%fused_computation.8.clone.1 | convolution fusion | flops 541589504 | bytes 2365953 | tf_op jit(solution)/shard_map/while/body/eval_jaxpr/dot_general | solution.py:55
  172.9 2.9 %fusion.29 = f32[2048,128]{1,0:T(8,128)S(1)} fusion(s32[1024]{0:T(1024)S(1)} %bitcast.24, bf16[1024]{0:T(1024)(128)(2,1)S(1)} %dynamic-slice_reduce_fusion.2, f32[2048,128]{1,0:T(8,128)S(1)} %get-tuple-element.107, pred[]{:T(512)S(6)} %compare.4, bf16[16,1024,128]{2,1,0:T(8,128)(2,1)} %get-tuple-element.117, s32[]{:T(128)} %get-tuple-element.106), kind=kOutput, calls=%fused_computation.8.clone.1 | convolution fusion | flops 541589504 | bytes 2365953 | tf_op jit(solution)/shard_map/while/body/eval_jaxpr/dot_general | solution.py:55
  175.9 2.9 %fusion.29 = f32[2048,128]{1,0:T(8,128)S(1)} fusion(s32[1024]{0:T(1024)S(1)} %bitcast.24, bf16[1024]{0:T(1024)(128)(2,1)S(1)} %dynamic-slice_reduce_fusion.2, f32[2048,128]{1,0:T(8,128)S(1)} %get-tuple-element.107, pred[]{:T(512)S(6)} %compare.4, bf16[16,1024,128]{2,1,0:T(8,128)(2,1)} %get-tuple-element.117, s32[]{:T(128)} %get-tuple-element.106), kind=kOutput, calls=%fused_computation.8.clone.1 | convolution fusion | flops 541589504 | bytes 2365953 | tf_op jit(solution)/shard_map/while/body/eval_jaxpr/dot_general | solution.py:55
  178.9 1.0 copy-done
  179.9 0.6 reduce-window.6
  180.5 0.2 slice_reduce_fusion
  180.8 1.4 scatter_custom_fusion
  182.3 1.9 gather_fusion.1
  184.2 0.7 all_to_all.6
  184.9 3.3 %all-to-all-start = ((f32[8,1,32]{2,1,0:T(1,128)}), f32[8,1,32]{2,1,0:T(1,128)S(1)}, u32[]{:S(2)}, u32[]{:S(2)}) async-start(f32[8,1,32]{2,1,0:T(1,128)} %all_to_all.6), calls=%async_computation | async-start | bytes 8192 | tf_op jit(solution)/shard_map/all_to_all | solution.py:64
  188.2 22.4 %psum.15 = f32[]{:T(128)} all-reduce(f32[]{:T(128)} %get-tuple-element.66), channel_id=1, replica_groups=mesh['rows'=8,'feat'=4] {'rows'}, use_global_device_ids=true, to_apply=%region_11.12 | all-reduce | flops 1 | bytes 8 | tf_op jit(solution)/shard_map/psum | solution.py:39
  211.3 0.5 broadcast.67
  211.8 0.7 reduce.10
  212.5 0.6 reshape.51
  213.1 29.8 %reduce-scatter.2.cloned.1.call-done = f32[256,128]{1,0:T(8,128)} async-done(((f32[2048,128]{1,0:T(8,128)}), f32[256,128]{1,0:T(8,128)}) %reduce-scatter.2.cloned.1.call-update) | async-done | bytes 131088 | tf_op jit(solution)/shard_map/reduce_scatter | solution.py:62
  (86 shorter events, 2.3 us)
Async XLA Ops:
  7.2 235.7 %reduce-scatter.2.cloned.1.call-start = ((), (), s32[]{:S(2)}) async-start(), calls=%async_computation.2 | async-start | bytes 1179648 | tf_op jit(solution)/shard_map/reduce_scatter | solution.py:62
  8.1 8.2 %collective-permute-start = (bf16[256,128]{1,0:T(8,128)(2,1)S(1)}, bf16[256,128]{1,0:T(8,128)(2,1)S(1)}, u32[]{:S(2)}, u32[]{:S(2)}) collective-permute-start(bf16[256,128]{1,0:T(8,128)(2,1)S(1)} %convert_element_type.23), channel_id=1, source_target_pairs={{0,4},{4,8},{8,12},{12,16},{16,20},{20,24},{24,28},{28,0},{1,5},{5... | collective-permute-start | bytes 196616 | tf_op jit(solution)/shard_map/ppermute | solution.py:17
  16.4 7.0 %collective-permute-start.1 = (bf16[256,128]{1,0:T(8,128)(2,1)S(1)}, bf16[256,128]{1,0:T(8,128)(2,1)S(1)}, u32[]{:S(2)}, u32[]{:S(2)}) collective-permute-start(bf16[256,128]{1,0:T(8,128)(2,1)S(1)} %collective-permute-done), channel_id=1, source_target_pairs={{0,4},{4,8},{8,12},{12,16},{16,20},{20,24},{24,28},{28,0},{1,5},{5... | collective-permute-start | bytes 196616 | tf_op jit(solution)/shard_map/ppermute | solution.py:17
  23.3 7.0 %collective-permute-start.2 = (bf16[256,128]{1,0:T(8,128)(2,1)S(1)}, bf16[256,128]{1,0:T(8,128)(2,1)S(1)}, u32[]{:S(2)}, u32[]{:S(2)}) collective-permute-start(bf16[256,128]{1,0:T(8,128)(2,1)S(1)} %collective-permute-done.1), channel_id=1, source_target_pairs={{0,4},{4,8},{8,12},{12,16},{16,20},{20,24},{24,28},{28,0},{1,5},{5... | collective-permute-start | bytes 196616 | tf_op jit(solution)/shard_map/ppermute | solution.py:17
  30.3 7.0 %collective-permute-start.3 = (bf16[256,128]{1,0:T(8,128)(2,1)S(1)}, bf16[256,128]{1,0:T(8,128)(2,1)S(1)}, u32[]{:S(2)}, u32[]{:S(2)}) collective-permute-start(bf16[256,128]{1,0:T(8,128)(2,1)S(1)} %collective-permute-done.2), channel_id=1, source_target_pairs={{0,4},{4,8},{8,12},{12,16},{16,20},{20,24},{24,28},{28,0},{1,5},{5... | collective-permute-start | bytes 196616 | tf_op jit(solution)/shard_map/ppermute | solution.py:17
  37.3 7.3 %collective-permute-start.4 = (bf16[256,128]{1,0:T(8,128)(2,1)S(1)}, bf16[256,128]{1,0:T(8,128)(2,1)S(1)}, u32[]{:S(2)}, u32[]{:S(2)}) collective-permute-start(bf16[256,128]{1,0:T(8,128)(2,1)S(1)} %collective-permute-done.3), channel_id=1, source_target_pairs={{0,4},{4,8},{8,12},{12,16},{16,20},{20,24},{24,28},{28,0},{1,5},{5... | collective-permute-start | bytes 196616 | tf_op jit(solution)/shard_map/ppermute | solution.py:17
  44.6 7.0 %collective-permute-start.5 = (bf16[256,128]{1,0:T(8,128)(2,1)S(1)}, bf16[256,128]{1,0:T(8,128)(2,1)S(1)}, u32[]{:S(2)}, u32[]{:S(2)}) collective-permute-start(bf16[256,128]{1,0:T(8,128)(2,1)S(1)} %collective-permute-done.4), channel_id=1, source_target_pairs={{0,4},{4,8},{8,12},{12,16},{16,20},{20,24},{24,28},{28,0},{1,5},{5... | collective-permute-start | bytes 196616 | tf_op jit(solution)/shard_map/ppermute | solution.py:17
  51.5 7.0 %collective-permute-start.6 = (bf16[256,128]{1,0:T(8,128)(2,1)S(1)}, bf16[256,128]{1,0:T(8,128)(2,1)S(1)}, u32[]{:S(2)}, u32[]{:S(2)}) collective-permute-start(bf16[256,128]{1,0:T(8,128)(2,1)S(1)} %collective-permute-done.5), channel_id=1, source_target_pairs={{0,4},{4,8},{8,12},{12,16},{16,20},{20,24},{24,28},{28,0},{1,5},{5... | collective-permute-start | bytes 196616 | tf_op jit(solution)/shard_map/ppermute | solution.py:17
  118.0 5.7 %copy-start.2 = (s32[256,1]{0,1:T(1,128)S(1)}, s32[256,1]{0,1:T(1,128)}, u32[]{:S(2)}) copy-start(s32[256,1]{0,1:T(1,128)} %param.10) | copy-start | bytes 3076
  118.0 11.6 %copy-start.3 = (s32[256]{0:T(256)S(1)}, s32[256]{0:T(256)}, u32[]{:S(2)}) copy-start(s32[256]{0:T(256)} %param.11) | copy-start | bytes 3076
  130.6 49.3 %copy-start.1 = (s32[256]{0:T(256)S(1)}, s32[256]{0:T(256)}, u32[]{:S(2)}) copy-start(s32[256]{0:T(256)} %param.12) | copy-start | bytes 3076
  178.8 1.0 copy-start
  184.9 26.4 %all-to-all-start = ((f32[8,1,32]{2,1,0:T(1,128)}), f32[8,1,32]{2,1,0:T(1,128)S(1)}, u32[]{:S(2)}, u32[]{:S(2)}) async-start(f32[8,1,32]{2,1,0:T(1,128)} %all_to_all.6), calls=%async_computation | async-start | bytes 8192 | tf_op jit(solution)/shard_map/all_to_all | solution.py:64
Sparse Core Ops, SparseCore 0:
  180.0 62.8 reduce-scatter.1
